TPU v7x, 128 devices: a whole 4x4x4 slice. The times are simulated.
128 devices in a mesh: dp: 2 (over core), tensor: 64 (over z, y, x).
Axes of the slice: x: 4, y: 4, z: 4, core: 2. Of those that a mesh axis runs over, the one named last changes fastest.
Arguments:
- resid_stream: bfloat16 [2048, 4608], P(('dp', 'tensor')), parts along dimension 0, may hold values from -120 to 120, as said below
- pre_gain: float32 [4608], replicated, may hold values from 0.5 to 1.5
- w_gate: bfloat16 [4608, 24576], P(None, 'tensor'), may hold values from -0.09375 to 0.09375
- w_up: bfloat16 [4608, 24576], P(None, 'tensor'), may hold values from -0.09375 to 0.09375
- w_down: bfloat16 [24576, 4608], P('tensor'), may hold values from -0.0390625 to 0.0390625
- post_gain: float32 [4608], replicated, may hold values from 0.5 to 1.5
Outputs:
- resid_out: bfloat16 [2048, 4608], P(('dp', 'tensor')), parts along dimension 0
There are 2 independent parts, one for each index of `dp`. A program takes and returns all parts, laid end to end along the dimension named above; an argument that names none is the same for every part. Nothing has to cross between parts.
Inputs may be any that keep to these rules, and one draw needn't show every extreme that they name: `resid_stream`: entries are real-valued.
All inputs are finite; a program needn't handle non-finite values.
Results may differ from a plain program's by a relative error of at most 0.0029.
Values may be sent and summed in bfloat16 or wider, within the bound.
No kernel may reach another device: no remote copies, remote signals or barrier semaphores. Data moves between devices by JAX's collectives and lax.ppermute only.
A program may use at most 128 MiB of HBM per device.

v0:
```python
import jax
import jax.numpy as jnp
from jax import lax
from jax.sharding import PartitionSpec as P


norm_eps = 1e-06
AXES = ("dp", "tensor")
STRIDE = (1, 4, 16)
ORDERS = ((0, 1, 2), (1, 2, 0), (2, 0, 1))
COLOURS = range(3)


def neighbour(dp, chip, axis, large):
    at = (chip // STRIDE[axis]) % 4
    wraps = large == (dp == 1) if axis == 0 else large == (dp == 0)
    to = at ^ 3 if wraps else at ^ 1
    return chip + (to - at) * STRIDE[axis]


def exchange(block, axis, large=True):
    perm = [(dp * 64 + t, dp * 64 + neighbour(dp, t, axis, large)) for dp in range(2) for t in range(64)]
    return lax.ppermute(block, AXES, perm)


def small_cubes():
    cubes, seen = [], set()
    for dp in range(2):
        for t in range(64):
            if (dp, t) in seen:
                continue
            cube = []
            for corner in range(8):
                chip = t
                for axis in range(3):
                    if corner >> axis & 1:
                        chip = neighbour(dp, chip, axis, False)
                cube.append(dp * 64 + chip)
                seen.add((dp, chip))
            cubes.append(cube)
    return cubes


def swap_in_cube(blocks):
    return lax.all_to_all(blocks, AXES, 0, 0, axis_index_groups=small_cubes(), tiled=True)


def block(resid_stream, pre_gain, w_gate, w_up, w_down, post_gain):
    rows, width = resid_stream.shape
    third = width // 3
    cols = [slice(c * third, (c + 1) * third) for c in COLOURS]
    bits = [tuple(1 << a for a in order) for order in ORDERS]
    stream = resid_stream.astype(jnp.float32)
    local_norm = stream * lax.rsqrt(jnp.mean(stream * stream, axis=1, keepdims=True) + norm_eps)
    normed = (local_norm * pre_gain).astype(jnp.bfloat16)

    cube_rows = swap_in_cube(jnp.broadcast_to(normed[None], (8, rows, width))).reshape(8 * rows, width)
    own = [cube_rows[:, cols[c]] for c in COLOURS]

    gate = [[] for _ in range(8)]
    up = [[] for _ in range(8)]

    def project(piece, colour, corners):
        g = jnp.dot(piece, w_gate[cols[colour]], preferred_element_type=jnp.float32)
        u = jnp.dot(piece, w_up[cols[colour]], preferred_element_type=jnp.float32)
        for i, corner in enumerate(corners):
            gate[corner].append(g[i * 8 * rows : (i + 1) * 8 * rows])
            up[corner].append(u[i * 8 * rows : (i + 1) * 8 * rows])

    first = [exchange(own[c], ORDERS[c][0]) for c in COLOURS]
    near = [jnp.concatenate([own[c], first[c]]) for c in COLOURS]
    second = [exchange(near[c], ORDERS[c][1]) for c in COLOURS]
    third_a = [exchange(near[c], ORDERS[c][2]) for c in COLOURS]
    third_b = [exchange(second[c], ORDERS[c][2]) for c in COLOURS]
    for pieces, base in (
        (near, lambda b: 0), (second, lambda b: b[1]), (third_a, lambda b: b[2]), (third_b, lambda b: b[1] + b[2])
    ):
        for c in COLOURS:
            at = base(bits[c])
            project(pieces[c], c, (at, at + bits[c][0]))
    hidden = [
        (jax.nn.gelu(sum(gate[k]), approximate=True) * sum(up[k])).astype(jnp.bfloat16) for k in range(8)
    ]

    def partial(colour, corners):
        both = jnp.concatenate([hidden[k] for k in corners]) if len(corners) > 1 else hidden[corners[0]]
        return jnp.dot(both, w_down[:, cols[colour]], preferred_element_type=jnp.float32)

    def send(sums, axis):
        return exchange(sums.astype(jnp.bfloat16), axis).astype(jnp.float32)

    far_a, far_b, far_c, mid, last, ends = [], [], [], [], [], []
    for c, (b0, b1, b2) in enumerate(bits):
        far_a.append(send(partial(c, (b1 + b2, 7)), ORDERS[c][2]))
        far_b.append(send(partial(c, (b0 + b2,)), ORDERS[c][2]))
        far_c.append(send(partial(c, (b2,)), ORDERS[c][2]))
    for c, (b0, b1, b2) in enumerate(bits):
        mid.append(send(partial(c, (b1, b1 + b0)) + far_a[c], ORDERS[c][1]))
    for c, (b0, b1, b2) in enumerate(bits):
        mine = partial(c, (0, b0))
        ends.append(send(mine[8 * rows :] + far_b[c] + mid[c][8 * rows :], ORDERS[c][0]))
        last.append(mine[: 8 * rows] + far_c[c] + mid[c][: 8 * rows])
    sums = jnp.concatenate([(last[c] + ends[c]).astype(jnp.bfloat16) for c in COLOURS], axis=1)

    block_rows = jnp.sum(swap_in_cube(sums.reshape(8, rows, width)).astype(jnp.float32), axis=0)

    row_factor = lax.rsqrt(jnp.mean(block_rows * block_rows, axis=1, keepdims=True) + norm_eps)
    post = (block_rows * row_factor * post_gain).astype(jnp.bfloat16)
    post = lax.optimization_barrier(post)
    return (stream + post.astype(jnp.float32)).astype(jnp.bfloat16)


def solution(mesh):
    return jax.shard_map(
        block,
        mesh=mesh,
        in_specs=(
            P(("dp", "tensor"), None),
            P(),
            P(None, "tensor"),
            P(None, "tensor"),
            P("tensor", None),
            P(),
        ),
        out_specs=P(("dp", "tensor"), None),
        check_vma=False,
    )
```

profile of v0, /device:TPU:0, one launch (start us, length us, event | category | flops | bytes accessed | tf_op | source)
XLA Modules:
  0.0 158.4 jit_solution(6707103697092384174)
XLA Ops:
  2.2 19.4 %all_to_all.10 = bf16[8,16,4608]{2,1,0:T(8,128)(2,1)S(1)} all-to-all(bf16[8,16,4608]{2,1,0:T(8,128)(2,1)S(1)} %broadcast_in_dim.2), channel_id=1, replica_groups={{0,3,4,7,16,19,20,23},{1,2,5,6,17,18,21,22},{8,11,12,15,24,27,28,31},{9..., dimensions={0} | all-to-all | bytes 2359296 | tf_op jit(solution)/shard_map/all_to_all | solution.py:45
  21.8 2.8 %collective-permute-start.2 = (bf16[128,1536]{1,0:T(8,128)(2,1)S(1)}, bf16[128,1536]{1,0:T(8,128)(2,1)S(1)}, u32[]{:S(2)}, u32[]{:S(2)}) collective-permute-start(bf16[128,1536]{1,0:T(8,128)(2,1)S(1)} %get-tuple-element.6), channel_id=1, source_target_pairs={{0,48},{1,49},{2,50},{3,51},{4,52},{5,53},{6,54},{7,55},{8,56},{9,... | collective-permute-start | bytes 1179656 | tf_op jit(solution)/shard_map/ppermute | solution.py:23
  24.5 2.0 %collective-permute-start.1 = (bf16[128,1536]{1,0:T(8,128)(2,1)S(1)}, bf16[128,1536]{1,0:T(8,128)(2,1)S(1)}, u32[]{:S(2)}, u32[]{:S(2)}) collective-permute-start(bf16[128,1536]{1,0:T(8,128)(2,1)S(1)} %get-tuple-element.7), channel_id=1, source_target_pairs={{0,12},{1,13},{2,14},{3,15},{4,8},{5,9},{6,10},{7,11},{8,4},{9,5},... | collective-permute-start | bytes 1179656 | tf_op jit(solution)/shard_map/ppermute | solution.py:23
  26.5 3.0 %collective-permute-done = bf16[128,1536]{1,0:T(8,128)(2,1)S(1)} collective-permute-done((bf16[128,1536]{1,0:T(8,128)(2,1)S(1)}, bf16[128,1536]{1,0:T(8,128)(2,1)S(1)}, u32[]{:S(2)}, u32[]{:S(2)}) %collective-permute-start) | collective-permute-done | bytes 393248 | tf_op jit(solution)/shard_map/ppermute | solution.py:23
  29.6 1.9 %collective-permute-start.8 = (bf16[256,1536]{1,0:T(8,128)(2,1)S(1)}, bf16[256,1536]{1,0:T(8,128)(2,1)S(1)}, u32[]{:S(2)}, u32[]{:S(2)}) collective-permute-start(bf16[256,1536]{1,0:T(8,128)(2,1)S(1)} %pad_maximum_fusion.1), channel_id=1, source_target_pairs={{0,12},{1,13},{2,14},{3,15},{4,8},{5,9},{6,10},{7,11},{8,4},{9,5},... | collective-permute-start | bytes 2359304 | tf_op jit(solution)/shard_map/ppermute | solution.py:23
  31.5 2.9 %collective-permute-start.6 = (bf16[256,1536]{1,0:T(8,128)(2,1)S(1)}, bf16[256,1536]{1,0:T(8,128)(2,1)S(1)}, u32[]{:S(2)}, u32[]{:S(2)}) collective-permute-start(bf16[256,1536]{1,0:T(8,128)(2,1)S(1)} %pad_maximum_fusion.1), channel_id=1, source_target_pairs={{0,48},{1,49},{2,50},{3,51},{4,52},{5,53},{6,54},{7,55},{8,56},{9,... | collective-permute-start | bytes 2359304 | tf_op jit(solution)/shard_map/ppermute | solution.py:23
  35.8 1.9 %collective-permute-start.5 = (bf16[256,1536]{1,0:T(8,128)(2,1)S(1)}, bf16[256,1536]{1,0:T(8,128)(2,1)S(1)}, u32[]{:S(2)}, u32[]{:S(2)}) collective-permute-start(bf16[256,1536]{1,0:T(8,128)(2,1)S(1)} %pad_maximum_fusion.2), channel_id=1, source_target_pairs={{0,48},{1,49},{2,50},{3,51},{4,52},{5,53},{6,54},{7,55},{8,56},{9,... | collective-permute-start | bytes 2359304 | tf_op jit(solution)/shard_map/ppermute | solution.py:23
  42.1 11.1 %collective-permute-done.5 = bf16[256,1536]{1,0:T(8,128)(2,1)S(1)} collective-permute-done((bf16[256,1536]{1,0:T(8,128)(2,1)S(1)}, bf16[256,1536]{1,0:T(8,128)(2,1)S(1)}, u32[]{:S(2)}, u32[]{:S(2)}) %collective-permute-start.5) | collective-permute-done | bytes 786464 | tf_op jit(solution)/shard_map/ppermute | solution.py:23
  58.1 1.7 %copy-done = bf16[384,4608]{1,0:T(8,128)(2,1)S(1)} copy-done((bf16[384,4608]{1,0:T(8,128)(2,1)S(1)}, bf16[384,4608]{1,0:T(8,128)(2,1)}, u32[]{:S(2)}) %copy-start) | copy-done | bytes 3538968
  60.1 2.9 %collective-permute-start.7 = (bf16[128,1536]{1,0:T(8,128)(2,1)S(1)}, bf16[128,1536]{1,0:T(8,128)(2,1)S(1)}, u32[]{:S(2)}, u32[]{:S(2)}) collective-permute-start(bf16[128,1536]{1,0:T(8,128)(2,1)S(1)} %convolution_convert_fusion.8), channel_id=1, source_target_pairs={{0,48},{1,49},{2,50},{3,51},{4,52},{5,53},{6,54},{7,55},{8,56},{9,... | collective-permute-start | bytes 1179656 | tf_op jit(solution)/shard_map/ppermute | solution.py:23
  63.1 2.0 %collective-permute-start.12 = (bf16[256,1536]{1,0:T(8,128)(2,1)S(1)}, bf16[256,1536]{1,0:T(8,128)(2,1)S(1)}, u32[]{:S(2)}, u32[]{:S(2)}) collective-permute-start(bf16[256,1536]{1,0:T(8,128)(2,1)S(1)} %collective-permute-done.5), channel_id=1, source_target_pairs={{0,1},{1,0},{2,3},{3,2},{4,5},{5,4},{6,7},{7,6},{8,9},{9,8},{10,11... | collective-permute-start | bytes 2359304 | tf_op jit(solution)/shard_map/ppermute | solution.py:23
  70.7 8.0 %collective-permute-done.10 = bf16[256,1536]{1,0:T(8,128)(2,1)S(1)} collective-permute-done((bf16[256,1536]{1,0:T(8,128)(2,1)S(1)}, bf16[256,1536]{1,0:T(8,128)(2,1)S(1)}, u32[]{:S(2)}, u32[]{:S(2)}) %collective-permute-start.10) | collective-permute-done | bytes 786464 | tf_op jit(solution)/shard_map/ppermute | solution.py:23
  84.0 2.9 %collective-permute-start.13 = (bf16[256,1536]{1,0:T(8,128)(2,1)S(1)}, bf16[256,1536]{1,0:T(8,128)(2,1)S(1)}, u32[]{:S(2)}, u32[]{:S(2)}) collective-permute-start(bf16[256,1536]{1,0:T(8,128)(2,1)S(1)} %convolution_convert_fusion.2), channel_id=1, source_target_pairs={{0,48},{1,49},{2,50},{3,51},{4,52},{5,53},{6,54},{7,55},{8,56},{9,... | collective-permute-start | bytes 2359304 | tf_op jit(solution)/shard_map/ppermute | solution.py:23
  88.1 1.5 collective-permute-start.23
  90.0 7.3 %collective-permute-done.13 = bf16[256,1536]{1,0:T(8,128)(2,1)S(1)} collective-permute-done((bf16[256,1536]{1,0:T(8,128)(2,1)S(1)}, bf16[256,1536]{1,0:T(8,128)(2,1)S(1)}, u32[]{:S(2)}, u32[]{:S(2)}) %collective-permute-start.13) | collective-permute-done | bytes 786464 | tf_op jit(solution)/shard_map/ppermute | solution.py:23
  97.9 1.5 collective-permute-start.14
  100.0 2.9 %collective-permute-start.19 = (bf16[256,1536]{1,0:T(8,128)(2,1)S(1)}, bf16[256,1536]{1,0:T(8,128)(2,1)S(1)}, u32[]{:S(2)}, u32[]{:S(2)}) collective-permute-start(bf16[256,1536]{1,0:T(8,128)(2,1)S(1)} %add_convert_fusion.1), channel_id=1, source_target_pairs={{0,48},{1,49},{2,50},{3,51},{4,52},{5,53},{6,54},{7,55},{8,56},{9,... | collective-permute-start | bytes 2359304 | tf_op jit(solution)/shard_map/ppermute | solution.py:23
  105.4 5.7 %collective-permute-done.14 = bf16[256,1536]{1,0:T(8,128)(2,1)S(1)} collective-permute-done((bf16[256,1536]{1,0:T(8,128)(2,1)S(1)}, bf16[256,1536]{1,0:T(8,128)(2,1)S(1)}, u32[]{:S(2)}, u32[]{:S(2)}) %collective-permute-start.14) | collective-permute-done | bytes 786464 | tf_op jit(solution)/shard_map/ppermute | solution.py:23
  113.7 1.7 %collective-permute-done.24 = bf16[256,1536]{1,0:T(8,128)(2,1)S(1)} collective-permute-done((bf16[256,1536]{1,0:T(8,128)(2,1)S(1)}, bf16[256,1536]{1,0:T(8,128)(2,1)S(1)}, u32[]{:S(2)}, u32[]{:S(2)}) %collective-permute-start.24) | collective-permute-done | bytes 786464 | tf_op jit(solution)/shard_map/ppermute | solution.py:23
  117.9 3.1 %collective-permute-done.20 = bf16[128,1536]{1,0:T(8,128)(2,1)S(1)} collective-permute-done((bf16[128,1536]{1,0:T(8,128)(2,1)S(1)}, bf16[128,1536]{1,0:T(8,128)(2,1)S(1)}, u32[]{:S(2)}, u32[]{:S(2)}) %collective-permute-start.20) | collective-permute-done | bytes 393248 | tf_op jit(solution)/shard_map/ppermute | solution.py:23
  121.5 3.9 %collective-permute-done.25 = bf16[128,1536]{1,0:T(8,128)(2,1)S(1)} collective-permute-done((bf16[128,1536]{1,0:T(8,128)(2,1)S(1)}, bf16[128,1536]{1,0:T(8,128)(2,1)S(1)}, u32[]{:S(2)}, u32[]{:S(2)}) %collective-permute-start.25) | collective-permute-done | bytes 393248 | tf_op jit(solution)/shard_map/ppermute | solution.py:23
  127.0 2.8 %collective-permute-start.26 = (bf16[128,1536]{1,0:T(8,128)(2,1)S(1)}, bf16[128,1536]{1,0:T(8,128)(2,1)S(1)}, u32[]{:S(2)}, u32[]{:S(2)}) collective-permute-start(bf16[128,1536]{1,0:T(8,128)(2,1)S(1)} %fusion), channel_id=1, source_target_pairs={{0,48},{1,49},{2,50},{3,51},{4,52},{5,53},{6,54},{7,55},{8,56},{9,... | collective-permute-start | bytes 1179656 | tf_op jit(solution)/shard_map/ppermute | solution.py:23
  129.9 10.7 %collective-permute-done.21 = bf16[128,1536]{1,0:T(8,128)(2,1)S(1)} collective-permute-done((bf16[128,1536]{1,0:T(8,128)(2,1)S(1)}, bf16[128,1536]{1,0:T(8,128)(2,1)S(1)}, u32[]{:S(2)}, u32[]{:S(2)}) %collective-permute-start.21) | collective-permute-done | bytes 393248 | tf_op jit(solution)/shard_map/ppermute | solution.py:23
  141.3 15.5 %all_to_all.11 = bf16[8,16,4608]{2,1,0:T(8,128)(2,1)S(1)} all-to-all(bf16[8,16,4608]{2,1,0:T(8,128)(2,1)S(1)} %bitcast.27), channel_id=1, replica_groups={{0,3,4,7,16,19,20,23},{1,2,5,6,17,18,21,22},{8,11,12,15,24,27,28,31},{9..., dimensions={0} | all-to-all | bytes 2359296 | tf_op jit(solution)/shard_map/all_to_all | solution.py:45
  (107 shorter events, 39.0 us)
Async XLA Ops:
  21.8 12.6 %collective-permute-start.2 = (bf16[128,1536]{1,0:T(8,128)(2,1)S(1)}, bf16[128,1536]{1,0:T(8,128)(2,1)S(1)}, u32[]{:S(2)}, u32[]{:S(2)}) collective-permute-start(bf16[128,1536]{1,0:T(8,128)(2,1)S(1)} %get-tuple-element.6), channel_id=1, source_target_pairs={{0,48},{1,49},{2,50},{3,51},{4,52},{5,53},{6,54},{7,55},{8,56},{9,... | collective-permute-start | bytes 1179656 | tf_op jit(solution)/shard_map/ppermute | solution.py:23
  24.5 11.2 %collective-permute-start.1 = (bf16[128,1536]{1,0:T(8,128)(2,1)S(1)}, bf16[128,1536]{1,0:T(8,128)(2,1)S(1)}, u32[]{:S(2)}, u32[]{:S(2)}) collective-permute-start(bf16[128,1536]{1,0:T(8,128)(2,1)S(1)} %get-tuple-element.7), channel_id=1, source_target_pairs={{0,12},{1,13},{2,14},{3,15},{4,8},{5,9},{6,10},{7,11},{8,4},{9,5},... | collective-permute-start | bytes 1179656 | tf_op jit(solution)/shard_map/ppermute | solution.py:23
  29.6 24.7 %collective-permute-start.8 = (bf16[256,1536]{1,0:T(8,128)(2,1)S(1)}, bf16[256,1536]{1,0:T(8,128)(2,1)S(1)}, u32[]{:S(2)}, u32[]{:S(2)}) collective-permute-start(bf16[256,1536]{1,0:T(8,128)(2,1)S(1)} %pad_maximum_fusion.1), channel_id=1, source_target_pairs={{0,12},{1,13},{2,14},{3,15},{4,8},{5,9},{6,10},{7,11},{8,4},{9,5},... | collective-permute-start | bytes 2359304 | tf_op jit(solution)/shard_map/ppermute | solution.py:23
  31.5 25.1 %collective-permute-start.6 = (bf16[256,1536]{1,0:T(8,128)(2,1)S(1)}, bf16[256,1536]{1,0:T(8,128)(2,1)S(1)}, u32[]{:S(2)}, u32[]{:S(2)}) collective-permute-start(bf16[256,1536]{1,0:T(8,128)(2,1)S(1)} %pad_maximum_fusion.1), channel_id=1, source_target_pairs={{0,48},{1,49},{2,50},{3,51},{4,52},{5,53},{6,54},{7,55},{8,56},{9,... | collective-permute-start | bytes 2359304 | tf_op jit(solution)/shard_map/ppermute | solution.py:23
  34.4 21.0 %collective-permute-start.9 = (bf16[256,1536]{1,0:T(8,128)(2,1)S(1)}, bf16[256,1536]{1,0:T(8,128)(2,1)S(1)}, u32[]{:S(2)}, u32[]{:S(2)}) collective-permute-start(bf16[256,1536]{1,0:T(8,128)(2,1)S(1)} %pad_maximum_fusion.3), channel_id=1, source_target_pairs={{0,12},{1,13},{2,14},{3,15},{4,8},{5,9},{6,10},{7,11},{8,4},{9,5},... | collective-permute-start | bytes 2359304 | tf_op jit(solution)/shard_map/ppermute | solution.py:23
  35.7 29.7 %collective-permute-start.3 = (bf16[256,1536]{1,0:T(8,128)(2,1)S(1)}, bf16[256,1536]{1,0:T(8,128)(2,1)S(1)}, u32[]{:S(2)}, u32[]{:S(2)}) collective-permute-start(bf16[256,1536]{1,0:T(8,128)(2,1)S(1)} %pad_maximum_fusion.3), channel_id=1, source_target_pairs={{0,1},{1,0},{2,3},{3,2},{4,5},{5,4},{6,7},{7,6},{8,9},{9,8},{10,11... | collective-permute-start | bytes 2359304 | tf_op jit(solution)/shard_map/ppermute | solution.py:23
  35.8 17.3 %collective-permute-start.5 = (bf16[256,1536]{1,0:T(8,128)(2,1)S(1)}, bf16[256,1536]{1,0:T(8,128)(2,1)S(1)}, u32[]{:S(2)}, u32[]{:S(2)}) collective-permute-start(bf16[256,1536]{1,0:T(8,128)(2,1)S(1)} %pad_maximum_fusion.2), channel_id=1, source_target_pairs={{0,48},{1,49},{2,50},{3,51},{4,52},{5,53},{6,54},{7,55},{8,56},{9,... | collective-permute-start | bytes 2359304 | tf_op jit(solution)/shard_map/ppermute | solution.py:23
  53.1 15.5 %collective-permute-start.4 = (bf16[256,1536]{1,0:T(8,128)(2,1)S(1)}, bf16[256,1536]{1,0:T(8,128)(2,1)S(1)}, u32[]{:S(2)}, u32[]{:S(2)}) collective-permute-start(bf16[256,1536]{1,0:T(8,128)(2,1)S(1)} %pad_maximum_fusion.2), channel_id=1, source_target_pairs={{0,1},{1,0},{2,3},{3,2},{4,5},{5,4},{6,7},{7,6},{8,9},{9,8},{10,11... | collective-permute-start | bytes 2359304 | tf_op jit(solution)/shard_map/ppermute | solution.py:23
  60.1 66.8 %collective-permute-start.7 = (bf16[128,1536]{1,0:T(8,128)(2,1)S(1)}, bf16[128,1536]{1,0:T(8,128)(2,1)S(1)}, u32[]{:S(2)}, u32[]{:S(2)}) collective-permute-start(bf16[128,1536]{1,0:T(8,128)(2,1)S(1)} %convolution_convert_fusion.8), channel_id=1, source_target_pairs={{0,48},{1,49},{2,50},{3,51},{4,52},{5,53},{6,54},{7,55},{8,56},{9,... | collective-permute-start | bytes 1179656 | tf_op jit(solution)/shard_map/ppermute | solution.py:23
  63.1 16.8 %collective-permute-start.12 = (bf16[256,1536]{1,0:T(8,128)(2,1)S(1)}, bf16[256,1536]{1,0:T(8,128)(2,1)S(1)}, u32[]{:S(2)}, u32[]{:S(2)}) collective-permute-start(bf16[256,1536]{1,0:T(8,128)(2,1)S(1)} %collective-permute-done.5), channel_id=1, source_target_pairs={{0,1},{1,0},{2,3},{3,2},{4,5},{5,4},{6,7},{7,6},{8,9},{9,8},{10,11... | collective-permute-start | bytes 2359304 | tf_op jit(solution)/shard_map/ppermute | solution.py:23
  65.1 15.9 %collective-permute-start.11 = (bf16[256,1536]{1,0:T(8,128)(2,1)S(1)}, bf16[256,1536]{1,0:T(8,128)(2,1)S(1)}, u32[]{:S(2)}, u32[]{:S(2)}) collective-permute-start(bf16[256,1536]{1,0:T(8,128)(2,1)S(1)} %collective-permute-done.8), channel_id=1, source_target_pairs={{0,48},{1,49},{2,50},{3,51},{4,52},{5,53},{6,54},{7,55},{8,56},{9,... | collective-permute-start | bytes 2359304 | tf_op jit(solution)/shard_map/ppermute | solution.py:23
  65.5 13.2 %collective-permute-start.10 = (bf16[256,1536]{1,0:T(8,128)(2,1)S(1)}, bf16[256,1536]{1,0:T(8,128)(2,1)S(1)}, u32[]{:S(2)}, u32[]{:S(2)}) collective-permute-start(bf16[256,1536]{1,0:T(8,128)(2,1)S(1)} %collective-permute-done.3), channel_id=1, source_target_pairs={{0,12},{1,13},{2,14},{3,15},{4,8},{5,9},{6,10},{7,11},{8,4},{9,5},... | collective-permute-start | bytes 2359304 | tf_op jit(solution)/shard_map/ppermute | solution.py:23
  84.0 13.3 %collective-permute-start.13 = (bf16[256,1536]{1,0:T(8,128)(2,1)S(1)}, bf16[256,1536]{1,0:T(8,128)(2,1)S(1)}, u32[]{:S(2)}, u32[]{:S(2)}) collective-permute-start(bf16[256,1536]{1,0:T(8,128)(2,1)S(1)} %convolution_convert_fusion.2), channel_id=1, source_target_pairs={{0,48},{1,49},{2,50},{3,51},{4,52},{5,53},{6,54},{7,55},{8,56},{9,... | collective-permute-start | bytes 2359304 | tf_op jit(solution)/shard_map/ppermute | solution.py:23
  87.0 29.3 %collective-permute-start.15 = (bf16[128,1536]{1,0:T(8,128)(2,1)S(1)}, bf16[128,1536]{1,0:T(8,128)(2,1)S(1)}, u32[]{:S(2)}, u32[]{:S(2)}) collective-permute-start(bf16[128,1536]{1,0:T(8,128)(2,1)S(1)} %convolution_convert_fusion.7), channel_id=1, source_target_pairs={{0,48},{1,49},{2,50},{3,51},{4,52},{5,53},{6,54},{7,55},{8,56},{9,... | collective-permute-start | bytes 1179656 | tf_op jit(solution)/shard_map/ppermute | solution.py:23
  87.4 12.0 %collective-permute-start.18 = (bf16[256,1536]{1,0:T(8,128)(2,1)S(1)}, bf16[256,1536]{1,0:T(8,128)(2,1)S(1)}, u32[]{:S(2)}, u32[]{:S(2)}) collective-permute-start(bf16[256,1536]{1,0:T(8,128)(2,1)S(1)} %convolution_convert_fusion.1), channel_id=1, source_target_pairs={{0,1},{1,0},{2,3},{3,2},{4,5},{5,4},{6,7},{7,6},{8,9},{9,8},{10,11... | collective-permute-start | bytes 2359304 | tf_op jit(solution)/shard_map/ppermute | solution.py:23
  88.1 14.7 %collective-permute-start.23 = (bf16[256,1536]{1,0:T(8,128)(2,1)S(1)}, bf16[256,1536]{1,0:T(8,128)(2,1)S(1)}, u32[]{:S(2)}, u32[]{:S(2)}) collective-permute-start(bf16[256,1536]{1,0:T(8,128)(2,1)S(1)} %convolution_convert_fusion), channel_id=1, source_target_pairs={{0,12},{1,13},{2,14},{3,15},{4,8},{5,9},{6,10},{7,11},{8,4},{9,5},... | collective-permute-start | bytes 2359304 | tf_op jit(solution)/shard_map/ppermute | solution.py:23
  97.9 13.3 %collective-permute-start.14 = (bf16[256,1536]{1,0:T(8,128)(2,1)S(1)}, bf16[256,1536]{1,0:T(8,128)(2,1)S(1)}, u32[]{:S(2)}, u32[]{:S(2)}) collective-permute-start(bf16[256,1536]{1,0:T(8,128)(2,1)S(1)} %add_convert_fusion.2), channel_id=1, source_target_pairs={{0,12},{1,13},{2,14},{3,15},{4,8},{5,9},{6,10},{7,11},{8,4},{9,5},... | collective-permute-start | bytes 2359304 | tf_op jit(solution)/shard_map/ppermute | solution.py:23
  100.0 13.3 %collective-permute-start.19 = (bf16[256,1536]{1,0:T(8,128)(2,1)S(1)}, bf16[256,1536]{1,0:T(8,128)(2,1)S(1)}, u32[]{:S(2)}, u32[]{:S(2)}) collective-permute-start(bf16[256,1536]{1,0:T(8,128)(2,1)S(1)} %add_convert_fusion.1), channel_id=1, source_target_pairs={{0,48},{1,49},{2,50},{3,51},{4,52},{5,53},{6,54},{7,55},{8,56},{9,... | collective-permute-start | bytes 2359304 | tf_op jit(solution)/shard_map/ppermute | solution.py:23
  103.4 12.1 %collective-permute-start.24 = (bf16[256,1536]{1,0:T(8,128)(2,1)S(1)}, bf16[256,1536]{1,0:T(8,128)(2,1)S(1)}, u32[]{:S(2)}, u32[]{:S(2)}) collective-permute-start(bf16[256,1536]{1,0:T(8,128)(2,1)S(1)} %add_convert_fusion), channel_id=1, source_target_pairs={{0,1},{1,0},{2,3},{3,2},{4,5},{5,4},{6,7},{7,6},{8,9},{9,8},{10,11... | collective-permute-start | bytes 2359304 | tf_op jit(solution)/shard_map/ppermute | solution.py:23
  111.2 29.7 %collective-permute-start.22 = (bf16[128,1536]{1,0:T(8,128)(2,1)S(1)}, bf16[128,1536]{1,0:T(8,128)(2,1)S(1)}, u32[]{:S(2)}, u32[]{:S(2)}) collective-permute-start(bf16[128,1536]{1,0:T(8,128)(2,1)S(1)} %convolution_convert_fusion.4), channel_id=1, source_target_pairs={{0,12},{1,13},{2,14},{3,15},{4,8},{5,9},{6,10},{7,11},{8,4},{9,5},... | collective-permute-start | bytes 1179656 | tf_op jit(solution)/shard_map/ppermute | solution.py:23
  115.5 14.4 %collective-permute-start.17 = (bf16[128,1536]{1,0:T(8,128)(2,1)S(1)}, bf16[128,1536]{1,0:T(8,128)(2,1)S(1)}, u32[]{:S(2)}, u32[]{:S(2)}) collective-permute-start(bf16[128,1536]{1,0:T(8,128)(2,1)S(1)} %convolution_convert_fusion.6), channel_id=1, source_target_pairs={{0,1},{1,0},{2,3},{3,2},{4,5},{5,4},{6,7},{7,6},{8,9},{9,8},{10,11... | collective-permute-start | bytes 1179656 | tf_op jit(solution)/shard_map/ppermute | solution.py:23
  116.3 9.1 %collective-permute-start.25 = (bf16[128,1536]{1,0:T(8,128)(2,1)S(1)}, bf16[128,1536]{1,0:T(8,128)(2,1)S(1)}, u32[]{:S(2)}, u32[]{:S(2)}) collective-permute-start(bf16[128,1536]{1,0:T(8,128)(2,1)S(1)} %convolution_convert_fusion.3), channel_id=1, source_target_pairs={{0,12},{1,13},{2,14},{3,15},{4,8},{5,9},{6,10},{7,11},{8,4},{9,5},... | collective-permute-start | bytes 1179656 | tf_op jit(solution)/shard_map/ppermute | solution.py:23
  125.4 15.3 %collective-permute-start.21 = (bf16[128,1536]{1,0:T(8,128)(2,1)S(1)}, bf16[128,1536]{1,0:T(8,128)(2,1)S(1)}, u32[]{:S(2)}, u32[]{:S(2)}) collective-permute-start(bf16[128,1536]{1,0:T(8,128)(2,1)S(1)} %fusion.3), channel_id=1, source_target_pairs={{0,12},{1,13},{2,14},{3,15},{4,8},{5,9},{6,10},{7,11},{8,4},{9,5},... | collective-permute-start | bytes 1179656 | tf_op jit(solution)/shard_map/ppermute | solution.py:23
  127.0 14.1 %collective-permute-start.26 = (bf16[128,1536]{1,0:T(8,128)(2,1)S(1)}, bf16[128,1536]{1,0:T(8,128)(2,1)S(1)}, u32[]{:S(2)}, u32[]{:S(2)}) collective-permute-start(bf16[128,1536]{1,0:T(8,128)(2,1)S(1)} %fusion), channel_id=1, source_target_pairs={{0,48},{1,49},{2,50},{3,51},{4,52},{5,53},{6,54},{7,55},{8,56},{9,... | collective-permute-start | bytes 1179656 | tf_op jit(solution)/shard_map/ppermute | solution.py:23
  (8 other events, 53.3 us)
where the time goes:
time: 159 us; the launch traced here: 158 us
  waiting for transfers between devices  55.1 us (35%)
  starting transfers between devices  37.8 us (24%)
  blocking collectives  34.9 us (22%)
  matrix products  21.1 us (13%)
  other arithmetic  5.87 us (4%)
  local copies, waits for them, and re-layouts  3.17 us (2%)
    ppermute x27, waiting for transfers between devices, exchange(): return lax.ppermute(block, AXES, perm)  55.1 us
    ppermute x27, starting transfers between devices, exchange(): return lax.ppermute(block, AXES, perm)  37.8 us
    all_to_all x2, blocking collectives, swap_in_cube(): lax.all_to_all(blocks, AXES, 0, 0, axis_index_groups=small_cubes(), tiled...  34.9 us
    dot_general x15, matrix products, partial(): jnp.dot(both, w_down[:, cols[colour]], preferred_element_type=jnp.float32)  7.31 us
    dot_general x12, matrix products, project(): g = jnp.dot(piece, w_gate[cols[colour]], preferred_element_type=jnp.float32)  6.9 us
    dot_general x12, matrix products, project(): u = jnp.dot(piece, w_up[cols[colour]], preferred_element_type=jnp.float32)  6.88 us
  transfers between devices with their start and end apart: 27, of which 11 were waited for; matrix products, arithmetic and copies ran while one was open for 15% of the time, Pallas kernels for 0%

commit v1 on v0

--- a/solution.py
+++ b/solution.py
@@ -45,7 +45,7 @@
     return lax.all_to_all(blocks, AXES, 0, 0, axis_index_groups=small_cubes(), tiled=True)
 
 
-def block(resid_stream, pre_gain, w_gate, w_up, w_down, post_gain):
+def forward(resid_stream, pre_gain, w_gate, w_up, w_down, post_gain):
     rows, width = resid_stream.shape
     third = width // 3
     cols = [slice(c * third, (c + 1) * third) for c in COLOURS]
@@ -70,7 +70,11 @@
     first = [exchange(own[c], ORDERS[c][0]) for c in COLOURS]
     near = [jnp.concatenate([own[c], first[c]]) for c in COLOURS]
     second = [exchange(near[c], ORDERS[c][1]) for c in COLOURS]
-    third_a = [exchange(near[c], ORDERS[c][2]) for c in COLOURS]
+    third_o = [exchange(own[c], ORDERS[c][2]) for c in COLOURS]
+    third_f = [exchange(first[c], ORDERS[c][2]) for c in COLOURS]
+    third_a = []
+    for c in COLOURS:
+        third_a.append(jnp.concatenate([third_o[c], third_f[c]]))
     third_b = [exchange(second[c], ORDERS[c][2]) for c in COLOURS]
     for pieces, base in (
         (near, lambda b: 0), (second, lambda b: b[1]), (third_a, lambda b: b[2]), (third_b, lambda b: b[1] + b[2])
@@ -82,25 +86,33 @@
         (jax.nn.gelu(sum(gate[k]), approximate=True) * sum(up[k])).astype(jnp.bfloat16) for k in range(8)
     ]
 
+    down = []
+    for c in COLOURS:
+        down.append(lax.optimization_barrier(w_down[:, cols[c]]))
+
     def partial(colour, corners):
         both = jnp.concatenate([hidden[k] for k in corners]) if len(corners) > 1 else hidden[corners[0]]
-        return jnp.dot(both, w_down[:, cols[colour]], preferred_element_type=jnp.float32)
+        return jnp.dot(both, down[colour], preferred_element_type=jnp.float32)
 
     def send(sums, axis):
-        return exchange(sums.astype(jnp.bfloat16), axis).astype(jnp.float32)
+        return exchange(sums.astype(jnp.bfloat16), axis)
 
-    far_a, far_b, far_c, mid, last, ends = [], [], [], [], [], []
+    half = 8 * rows
+    wide = lambda piece: piece.astype(jnp.float32)
+    far_a, far_b, mid, edge, ends, last = [], [], [], [], [], []
     for c, (b0, b1, b2) in enumerate(bits):
         far_a.append(send(partial(c, (b1 + b2, 7)), ORDERS[c][2]))
-        far_b.append(send(partial(c, (b0 + b2,)), ORDERS[c][2]))
-        far_c.append(send(partial(c, (b2,)), ORDERS[c][2]))
+        far_b.append(send(partial(c, (b2, b0 + b2)), ORDERS[c][2]))
     for c, (b0, b1, b2) in enumerate(bits):
-        mid.append(send(partial(c, (b1, b1 + b0)) + far_a[c], ORDERS[c][1]))
+        mid.append(send(partial(c, (b1 + b0,)) + wide(far_a[c][half:]), ORDERS[c][1]))
+        edge.append(send(partial(c, (b1,)) + wide(far_a[c][:half]), ORDERS[c][1]))
     for c, (b0, b1, b2) in enumerate(bits):
         mine = partial(c, (0, b0))
-        ends.append(send(mine[8 * rows :] + far_b[c] + mid[c][8 * rows :], ORDERS[c][0]))
-        last.append(mine[: 8 * rows] + far_c[c] + mid[c][: 8 * rows])
-    sums = jnp.concatenate([(last[c] + ends[c]).astype(jnp.bfloat16) for c in COLOURS], axis=1)
+        ends.append(send(mine[half:] + wide(far_b[c][half:]) + wide(mid[c]), ORDERS[c][0]))
+        last.append(mine[:half] + wide(far_b[c][:half]) + wide(edge[c]))
+    met = lax.ppermute(mid[0][:rows, :128], "dp", [(0, 1), (1, 0)])
+    zero = 0.0 * wide(met[:1, :1])
+    sums = jnp.concatenate([(last[c] + wide(ends[c]) + zero).astype(jnp.bfloat16) for c in COLOURS], axis=1)
 
     block_rows = jnp.sum(swap_in_cube(sums.reshape(8, rows, width)).astype(jnp.float32), axis=0)
 
@@ -112,7 +124,7 @@
 
 def solution(mesh):
     return jax.shard_map(
-        block,
+        forward,
         mesh=mesh,
         in_specs=(
             P(("dp", "tensor"), None),

time: 159 us -> 162 us (1.019)
  starting transfers between devices: 37.8 us -> 44.9 us
  waiting for transfers between devices: 55.1 us -> 50.2 us
    ppermute x27 -> x30, starting transfers between devices: 37.8 us -> 44.9 us  [exchange(): return lax.ppermute(block, AXES, perm)]
    ppermute x27 -> x30, waiting for transfers between devices: 55.1 us -> 49.2 us  [exchange(): return lax.ppermute(block, AXES, perm)]
    convert_element_type x15 -> x12, other arithmetic: 4.25 us -> 3.75 us  [the longest x1 1.02 us: forward(): normed = (local_norm * pre_gain).astype(jnp.bfloat16)]
  transfers between devices with their start and end apart: 27 -> 31, of which waited for: 11 -> 14; matrix products, arithmetic and copies ran while one was open for 15% -> 12% of each run, Pallas kernels for 0% -> 0%
where the time goes in v1:
time: 162 us; the launch traced here: 161 us
  waiting for transfers between devices  50.2 us (31%)
  starting transfers between devices  44.9 us (28%)
  blocking collectives  35.2 us (22%)
  matrix products  21.2 us (13%)
  other arithmetic  5.36 us (3%)
  local copies, waits for them, and re-layouts  3.1 us (2%)
    ppermute x30, waiting for transfers between devices, exchange(): return lax.ppermute(block, AXES, perm)  49.2 us
    ppermute x30, starting transfers between devices, exchange(): return lax.ppermute(block, AXES, perm)  44.9 us
    all_to_all x2, blocking collectives, swap_in_cube(): lax.all_to_all(blocks, AXES, 0, 0, axis_index_groups=small_cubes(), tiled...  35.2 us
    dot_general x15, matrix products, partial(): return jnp.dot(both, down[colour], preferred_element_type=jnp.float32)  7.45 us
    dot_general x12, matrix products, project(): g = jnp.dot(piece, w_gate[cols[colour]], preferred_element_type=jnp.float32)  6.88 us
    dot_general x12, matrix products, project(): u = jnp.dot(piece, w_up[cols[colour]], preferred_element_type=jnp.float32)  6.88 us
  transfers between devices with their start and end apart: 31, of which 14 were waited for; matrix products, arithmetic and copies ran while one was open for 12% of the time, Pallas kernels for 0%

profile of v1, /device:TPU:0, one launch (start us, length us, event | category | flops | bytes accessed | tf_op | source)
XLA Modules:
  0.0 161.1 jit_solution(13305864184683500881)
XLA Ops:
  2.2 19.7 %all_to_all.10 = bf16[8,16,4608]{2,1,0:T(8,128)(2,1)S(1)} all-to-all(bf16[8,16,4608]{2,1,0:T(8,128)(2,1)S(1)} %broadcast_in_dim.2), channel_id=1, replica_groups={{0,3,4,7,16,19,20,23},{1,2,5,6,17,18,21,22},{8,11,12,15,24,27,28,31},{9..., dimensions={0} | all-to-all | bytes 2359296 | tf_op jit(solution)/shard_map/all_to_all | solution.py:45
  22.0 2.8 %collective-permute-start.2 = (bf16[128,1536]{1,0:T(8,128)(2,1)S(1)}, bf16[128,1536]{1,0:T(8,128)(2,1)S(1)}, u32[]{:S(2)}, u32[]{:S(2)}) collective-permute-start(bf16[128,1536]{1,0:T(8,128)(2,1)S(1)} %get-tuple-element.9), channel_id=1, source_target_pairs={{0,48},{1,49},{2,50},{3,51},{4,52},{5,53},{6,54},{7,55},{8,56},{9,... | collective-permute-start | bytes 1179656 | tf_op jit(solution)/shard_map/ppermute | solution.py:23
  24.7 2.0 %collective-permute-start.1 = (bf16[128,1536]{1,0:T(8,128)(2,1)S(1)}, bf16[128,1536]{1,0:T(8,128)(2,1)S(1)}, u32[]{:S(2)}, u32[]{:S(2)}) collective-permute-start(bf16[128,1536]{1,0:T(8,128)(2,1)S(1)} %get-tuple-element.10), channel_id=1, source_target_pairs={{0,12},{1,13},{2,14},{3,15},{4,8},{5,9},{6,10},{7,11},{8,4},{9,5},... | collective-permute-start | bytes 1179656 | tf_op jit(solution)/shard_map/ppermute | solution.py:23
  29.0 4.7 %collective-permute-done.1 = bf16[128,1536]{1,0:T(8,128)(2,1)S(1)} collective-permute-done((bf16[128,1536]{1,0:T(8,128)(2,1)S(1)}, bf16[128,1536]{1,0:T(8,128)(2,1)S(1)}, u32[]{:S(2)}, u32[]{:S(2)}) %collective-permute-start.1) | collective-permute-done | bytes 393248 | tf_op jit(solution)/shard_map/ppermute | solution.py:23
  35.3 1.8 %collective-permute-start.3 = (bf16[256,1536]{1,0:T(8,128)(2,1)S(1)}, bf16[256,1536]{1,0:T(8,128)(2,1)S(1)}, u32[]{:S(2)}, u32[]{:S(2)}) collective-permute-start(bf16[256,1536]{1,0:T(8,128)(2,1)S(1)} %pad_maximum_fusion.3), channel_id=1, source_target_pairs={{0,1},{1,0},{2,3},{3,2},{4,5},{5,4},{6,7},{7,6},{8,9},{9,8},{10,11... | collective-permute-start | bytes 2359304 | tf_op jit(solution)/shard_map/ppermute | solution.py:23
  39.8 1.9 %collective-permute-start.11 = (bf16[256,1536]{1,0:T(8,128)(2,1)S(1)}, bf16[256,1536]{1,0:T(8,128)(2,1)S(1)}, u32[]{:S(2)}, u32[]{:S(2)}) collective-permute-start(bf16[256,1536]{1,0:T(8,128)(2,1)S(1)} %pad_maximum_fusion.1), channel_id=1, source_target_pairs={{0,12},{1,13},{2,14},{3,15},{4,8},{5,9},{6,10},{7,11},{8,4},{9,5},... | collective-permute-start | bytes 2359304 | tf_op jit(solution)/shard_map/ppermute | solution.py:23
  42.3 2.9 %collective-permute-start.8 = (bf16[128,1536]{1,0:T(8,128)(2,1)S(1)}, bf16[128,1536]{1,0:T(8,128)(2,1)S(1)}, u32[]{:S(2)}, u32[]{:S(2)}) collective-permute-start(bf16[128,1536]{1,0:T(8,128)(2,1)S(1)} %collective-permute-done), channel_id=1, source_target_pairs={{0,48},{1,49},{2,50},{3,51},{4,52},{5,53},{6,54},{7,55},{8,56},{9,... | collective-permute-start | bytes 1179656 | tf_op jit(solution)/shard_map/ppermute | solution.py:23
  47.7 3.6 %collective-permute-done.8 = bf16[128,1536]{1,0:T(8,128)(2,1)S(1)} collective-permute-done((bf16[128,1536]{1,0:T(8,128)(2,1)S(1)}, bf16[128,1536]{1,0:T(8,128)(2,1)S(1)}, u32[]{:S(2)}, u32[]{:S(2)}) %collective-permute-start.8) | collective-permute-done | bytes 393248 | tf_op jit(solution)/shard_map/ppermute | solution.py:23
  51.3 2.0 %collective-permute-start.5 = (bf16[128,1536]{1,0:T(8,128)(2,1)S(1)}, bf16[128,1536]{1,0:T(8,128)(2,1)S(1)}, u32[]{:S(2)}, u32[]{:S(2)}) collective-permute-start(bf16[128,1536]{1,0:T(8,128)(2,1)S(1)} %collective-permute-done.1), channel_id=1, source_target_pairs={{0,1},{1,0},{2,3},{3,2},{4,5},{5,4},{6,7},{7,6},{8,9},{9,8},{10,11... | collective-permute-start | bytes 1179656 | tf_op jit(solution)/shard_map/ppermute | solution.py:23
  54.5 2.8 %collective-permute-done.13 = bf16[128,1536]{1,0:T(8,128)(2,1)S(1)} collective-permute-done((bf16[128,1536]{1,0:T(8,128)(2,1)S(1)}, bf16[128,1536]{1,0:T(8,128)(2,1)S(1)}, u32[]{:S(2)}, u32[]{:S(2)}) %collective-permute-start.13) | collective-permute-done | bytes 393248 | tf_op jit(solution)/shard_map/ppermute | solution.py:23
  60.3 2.2 %collective-permute-start.15 = (bf16[256,1536]{1,0:T(8,128)(2,1)S(1)}, bf16[256,1536]{1,0:T(8,128)(2,1)S(1)}, u32[]{:S(2)}, u32[]{:S(2)}) collective-permute-start(bf16[256,1536]{1,0:T(8,128)(2,1)S(1)} %collective-permute-done.3), channel_id=1, source_target_pairs={{0,12},{1,13},{2,14},{3,15},{4,8},{5,9},{6,10},{7,11},{8,4},{9,5},... | collective-permute-start | bytes 2359304 | tf_op jit(solution)/shard_map/ppermute | solution.py:23
  64.3 2.2 %collective-permute-start.14 = (bf16[256,1536]{1,0:T(8,128)(2,1)S(1)}, bf16[256,1536]{1,0:T(8,128)(2,1)S(1)}, u32[]{:S(2)}, u32[]{:S(2)}) collective-permute-start(bf16[256,1536]{1,0:T(8,128)(2,1)S(1)} %collective-permute-done.11), channel_id=1, source_target_pairs={{0,48},{1,49},{2,50},{3,51},{4,52},{5,53},{6,54},{7,55},{8,56},{9,... | collective-permute-start | bytes 2359304 | tf_op jit(solution)/shard_map/ppermute | solution.py:23
  70.2 9.9 %collective-permute-done.9 = bf16[256,1536]{1,0:T(8,128)(2,1)S(1)} collective-permute-done((bf16[256,1536]{1,0:T(8,128)(2,1)S(1)}, bf16[256,1536]{1,0:T(8,128)(2,1)S(1)}, u32[]{:S(2)}, u32[]{:S(2)}) %collective-permute-start.9) | collective-permute-done | bytes 786464 | tf_op jit(solution)/shard_map/ppermute | solution.py:23
  90.2 2.0 %collective-permute-start.22 = (bf16[256,1536]{1,0:T(8,128)(2,1)S(1)}, bf16[256,1536]{1,0:T(8,128)(2,1)S(1)}, u32[]{:S(2)}, u32[]{:S(2)}) collective-permute-start(bf16[256,1536]{1,0:T(8,128)(2,1)S(1)} %convolution_convert_fusion.2), channel_id=1, source_target_pairs={{0,1},{1,0},{2,3},{3,2},{4,5},{5,4},{6,7},{7,6},{8,9},{9,8},{10,11... | collective-permute-start | bytes 2359304 | tf_op jit(solution)/shard_map/ppermute | solution.py:23
  96.0 10.7 %collective-permute-done.16 = bf16[256,1536]{1,0:T(8,128)(2,1)S(1)} collective-permute-done((bf16[256,1536]{1,0:T(8,128)(2,1)S(1)}, bf16[256,1536]{1,0:T(8,128)(2,1)S(1)}, u32[]{:S(2)}, u32[]{:S(2)}) %collective-permute-start.16) | collective-permute-done | bytes 786464 | tf_op jit(solution)/shard_map/ppermute | solution.py:23
  110.0 2.0 %collective-permute-start.28 = (bf16[128,1536]{1,0:T(8,128)(2,1)S(1)}, bf16[128,1536]{1,0:T(8,128)(2,1)S(1)}, u32[]{:S(2)}, u32[]{:S(2)}) collective-permute-start(bf16[128,1536]{1,0:T(8,128)(2,1)S(1)} %get-tuple-element.15), channel_id=1, source_target_pairs={{0,1},{1,0},{2,3},{3,2},{4,5},{5,4},{6,7},{7,6},{8,9},{9,8},{10,11... | collective-permute-start | bytes 1179656 | tf_op jit(solution)/shard_map/ppermute | solution.py:23
  112.4 4.9 %collective-permute-done.18 = bf16[128,1536]{1,0:T(8,128)(2,1)S(1)} collective-permute-done((bf16[128,1536]{1,0:T(8,128)(2,1)S(1)}, bf16[128,1536]{1,0:T(8,128)(2,1)S(1)}, u32[]{:S(2)}, u32[]{:S(2)}) %collective-permute-start.18) | collective-permute-done | bytes 393248 | tf_op jit(solution)/shard_map/ppermute | solution.py:23
  117.3 1.9 %collective-permute-start.29 = (bf16[128,1536]{1,0:T(8,128)(2,1)S(1)}, bf16[128,1536]{1,0:T(8,128)(2,1)S(1)}, u32[]{:S(2)}, u32[]{:S(2)}) collective-permute-start(bf16[128,1536]{1,0:T(8,128)(2,1)S(1)} %get-tuple-element.16), channel_id=1, source_target_pairs={{0,1},{1,0},{2,3},{3,2},{4,5},{5,4},{6,7},{7,6},{8,9},{9,8},{10,11... | collective-permute-start | bytes 1179656 | tf_op jit(solution)/shard_map/ppermute | solution.py:23
  121.2 2.2 %collective-permute-start.23 = (bf16[128,1536]{1,0:T(8,128)(2,1)S(1)}, bf16[128,1536]{1,0:T(8,128)(2,1)S(1)}, u32[]{:S(2)}, u32[]{:S(2)}) collective-permute-start(bf16[128,1536]{1,0:T(8,128)(2,1)S(1)} %get-tuple-element.13), channel_id=1, source_target_pairs={{0,48},{1,49},{2,50},{3,51},{4,52},{5,53},{6,54},{7,55},{8,56},{9,... | collective-permute-start | bytes 1179656 | tf_op jit(solution)/shard_map/ppermute | solution.py:23
  123.3 5.5 %collective-permute-done.24 = bf16[128,1536]{1,0:T(8,128)(2,1)S(1)} collective-permute-done((bf16[128,1536]{1,0:T(8,128)(2,1)S(1)}, bf16[128,1536]{1,0:T(8,128)(2,1)S(1)}, u32[]{:S(2)}, u32[]{:S(2)}) %collective-permute-start.24) | collective-permute-done | bytes 393248 | tf_op jit(solution)/shard_map/ppermute | solution.py:23
  128.9 2.0 %collective-permute-start.17 = (bf16[128,1536]{1,0:T(8,128)(2,1)S(1)}, bf16[128,1536]{1,0:T(8,128)(2,1)S(1)}, u32[]{:S(2)}, u32[]{:S(2)}) collective-permute-start(bf16[128,1536]{1,0:T(8,128)(2,1)S(1)} %get-tuple-element.11), channel_id=1, source_target_pairs={{0,12},{1,13},{2,14},{3,15},{4,8},{5,9},{6,10},{7,11},{8,4},{9,5},... | collective-permute-start | bytes 1179656 | tf_op jit(solution)/shard_map/ppermute | solution.py:23
  135.9 2.0 %collective-permute-start.19 = (bf16[128,1536]{1,0:T(8,128)(2,1)S(1)}, bf16[128,1536]{1,0:T(8,128)(2,1)S(1)}, u32[]{:S(2)}, u32[]{:S(2)}) collective-permute-start(bf16[128,1536]{1,0:T(8,128)(2,1)S(1)} %fusion.13), channel_id=1, source_target_pairs={{0,1},{1,0},{2,3},{3,2},{4,5},{5,4},{6,7},{7,6},{8,9},{9,8},{10,11... | collective-permute-start | bytes 1179656 | tf_op jit(solution)/shard_map/ppermute | solution.py:23
  137.9 4.2 %collective-permute-done.25 = bf16[128,1536]{1,0:T(8,128)(2,1)S(1)} collective-permute-done((bf16[128,1536]{1,0:T(8,128)(2,1)S(1)}, bf16[128,1536]{1,0:T(8,128)(2,1)S(1)}, u32[]{:S(2)}, u32[]{:S(2)}) %collective-permute-start.25) | collective-permute-done | bytes 393248 | tf_op jit(solution)/shard_map/ppermute | solution.py:23
  144.0 15.5 %all_to_all.11 = bf16[8,16,4608]{2,1,0:T(8,128)(2,1)S(1)} all-to-all(bf16[8,16,4608]{2,1,0:T(8,128)(2,1)S(1)} %bitcast.43), channel_id=1, replica_groups={{0,3,4,7,16,19,20,23},{1,2,5,6,17,18,21,22},{8,11,12,15,24,27,28,31},{9..., dimensions={0} | all-to-all | bytes 2359296 | tf_op jit(solution)/shard_map/all_to_all | solution.py:45
  (121 shorter events, 48.5 us)
Async XLA Ops:
  22.0 11.8 %collective-permute-start.2 = (bf16[128,1536]{1,0:T(8,128)(2,1)S(1)}, bf16[128,1536]{1,0:T(8,128)(2,1)S(1)}, u32[]{:S(2)}, u32[]{:S(2)}) collective-permute-start(bf16[128,1536]{1,0:T(8,128)(2,1)S(1)} %get-tuple-element.9), channel_id=1, source_target_pairs={{0,48},{1,49},{2,50},{3,51},{4,52},{5,53},{6,54},{7,55},{8,56},{9,... | collective-permute-start | bytes 1179656 | tf_op jit(solution)/shard_map/ppermute | solution.py:23
  27.1 12.6 %collective-permute-start.7 = (bf16[128,1536]{1,0:T(8,128)(2,1)S(1)}, bf16[128,1536]{1,0:T(8,128)(2,1)S(1)}, u32[]{:S(2)}, u32[]{:S(2)}) collective-permute-start(bf16[128,1536]{1,0:T(8,128)(2,1)S(1)} %get-tuple-element.8), channel_id=1, source_target_pairs={{0,48},{1,49},{2,50},{3,51},{4,52},{5,53},{6,54},{7,55},{8,56},{9,... | collective-permute-start | bytes 1179656 | tf_op jit(solution)/shard_map/ppermute | solution.py:23
  27.6 14.7 %collective-permute-start.12 = (bf16[128,1536]{1,0:T(8,128)(2,1)S(1)}, bf16[128,1536]{1,0:T(8,128)(2,1)S(1)}, u32[]{:S(2)}, u32[]{:S(2)}) collective-permute-start(bf16[128,1536]{1,0:T(8,128)(2,1)S(1)} %get-tuple-element.9), channel_id=1, source_target_pairs={{0,12},{1,13},{2,14},{3,15},{4,8},{5,9},{6,10},{7,11},{8,4},{9,5},... | collective-permute-start | bytes 1179656 | tf_op jit(solution)/shard_map/ppermute | solution.py:23
  33.7 12.1 %collective-permute-start.4 = (bf16[128,1536]{1,0:T(8,128)(2,1)S(1)}, bf16[128,1536]{1,0:T(8,128)(2,1)S(1)}, u32[]{:S(2)}, u32[]{:S(2)}) collective-permute-start(bf16[128,1536]{1,0:T(8,128)(2,1)S(1)} %get-tuple-element.10), channel_id=1, source_target_pairs={{0,1},{1,0},{2,3},{3,2},{4,5},{5,4},{6,7},{7,6},{8,9},{9,8},{10,11... | collective-permute-start | bytes 1179656 | tf_op jit(solution)/shard_map/ppermute | solution.py:23
  33.8 34.2 %collective-permute-start.6 = (bf16[256,1536]{1,0:T(8,128)(2,1)S(1)}, bf16[256,1536]{1,0:T(8,128)(2,1)S(1)}, u32[]{:S(2)}, u32[]{:S(2)}) collective-permute-start(bf16[256,1536]{1,0:T(8,128)(2,1)S(1)} %pad_maximum_fusion.2), channel_id=1, source_target_pairs={{0,48},{1,49},{2,50},{3,51},{4,52},{5,53},{6,54},{7,55},{8,56},{9,... | collective-permute-start | bytes 2359304 | tf_op jit(solution)/shard_map/ppermute | solution.py:23
  35.3 25.0 %collective-permute-start.3 = (bf16[256,1536]{1,0:T(8,128)(2,1)S(1)}, bf16[256,1536]{1,0:T(8,128)(2,1)S(1)}, u32[]{:S(2)}, u32[]{:S(2)}) collective-permute-start(bf16[256,1536]{1,0:T(8,128)(2,1)S(1)} %pad_maximum_fusion.3), channel_id=1, source_target_pairs={{0,1},{1,0},{2,3},{3,2},{4,5},{5,4},{6,7},{7,6},{8,9},{9,8},{10,11... | collective-permute-start | bytes 2359304 | tf_op jit(solution)/shard_map/ppermute | solution.py:23
  39.8 23.9 %collective-permute-start.11 = (bf16[256,1536]{1,0:T(8,128)(2,1)S(1)}, bf16[256,1536]{1,0:T(8,128)(2,1)S(1)}, u32[]{:S(2)}, u32[]{:S(2)}) collective-permute-start(bf16[256,1536]{1,0:T(8,128)(2,1)S(1)} %pad_maximum_fusion.1), channel_id=1, source_target_pairs={{0,12},{1,13},{2,14},{3,15},{4,8},{5,9},{6,10},{7,11},{8,4},{9,5},... | collective-permute-start | bytes 2359304 | tf_op jit(solution)/shard_map/ppermute | solution.py:23
  42.3 9.1 %collective-permute-start.8 = (bf16[128,1536]{1,0:T(8,128)(2,1)S(1)}, bf16[128,1536]{1,0:T(8,128)(2,1)S(1)}, u32[]{:S(2)}, u32[]{:S(2)}) collective-permute-start(bf16[128,1536]{1,0:T(8,128)(2,1)S(1)} %collective-permute-done), channel_id=1, source_target_pairs={{0,48},{1,49},{2,50},{3,51},{4,52},{5,53},{6,54},{7,55},{8,56},{9,... | collective-permute-start | bytes 1179656 | tf_op jit(solution)/shard_map/ppermute | solution.py:23
  45.8 11.4 %collective-permute-start.13 = (bf16[128,1536]{1,0:T(8,128)(2,1)S(1)}, bf16[128,1536]{1,0:T(8,128)(2,1)S(1)}, u32[]{:S(2)}, u32[]{:S(2)}) collective-permute-start(bf16[128,1536]{1,0:T(8,128)(2,1)S(1)} %collective-permute-done.2), channel_id=1, source_target_pairs={{0,12},{1,13},{2,14},{3,15},{4,8},{5,9},{6,10},{7,11},{8,4},{9,5},... | collective-permute-start | bytes 1179656 | tf_op jit(solution)/shard_map/ppermute | solution.py:23
  60.3 20.9 %collective-permute-start.15 = (bf16[256,1536]{1,0:T(8,128)(2,1)S(1)}, bf16[256,1536]{1,0:T(8,128)(2,1)S(1)}, u32[]{:S(2)}, u32[]{:S(2)}) collective-permute-start(bf16[256,1536]{1,0:T(8,128)(2,1)S(1)} %collective-permute-done.3), channel_id=1, source_target_pairs={{0,12},{1,13},{2,14},{3,15},{4,8},{5,9},{6,10},{7,11},{8,4},{9,5},... | collective-permute-start | bytes 2359304 | tf_op jit(solution)/shard_map/ppermute | solution.py:23
  64.3 18.2 %collective-permute-start.14 = (bf16[256,1536]{1,0:T(8,128)(2,1)S(1)}, bf16[256,1536]{1,0:T(8,128)(2,1)S(1)}, u32[]{:S(2)}, u32[]{:S(2)}) collective-permute-start(bf16[256,1536]{1,0:T(8,128)(2,1)S(1)} %collective-permute-done.11), channel_id=1, source_target_pairs={{0,48},{1,49},{2,50},{3,51},{4,52},{5,53},{6,54},{7,55},{8,56},{9,... | collective-permute-start | bytes 2359304 | tf_op jit(solution)/shard_map/ppermute | solution.py:23
  68.0 12.1 %collective-permute-start.9 = (bf16[256,1536]{1,0:T(8,128)(2,1)S(1)}, bf16[256,1536]{1,0:T(8,128)(2,1)S(1)}, u32[]{:S(2)}, u32[]{:S(2)}) collective-permute-start(bf16[256,1536]{1,0:T(8,128)(2,1)S(1)} %collective-permute-done.6), channel_id=1, source_target_pairs={{0,1},{1,0},{2,3},{3,2},{4,5},{5,4},{6,7},{7,6},{8,9},{9,8},{10,11... | collective-permute-start | bytes 2359304 | tf_op jit(solution)/shard_map/ppermute | solution.py:23
  87.5 33.7 %collective-permute-start.21 = (bf16[256,1536]{1,0:T(8,128)(2,1)S(1)}, bf16[256,1536]{1,0:T(8,128)(2,1)S(1)}, u32[]{:S(2)}, u32[]{:S(2)}) collective-permute-start(bf16[256,1536]{1,0:T(8,128)(2,1)S(1)} %convolution_convert_fusion.3), channel_id=1, source_target_pairs={{0,1},{1,0},{2,3},{3,2},{4,5},{5,4},{6,7},{7,6},{8,9},{9,8},{10,11... | collective-permute-start | bytes 2359304 | tf_op jit(solution)/shard_map/ppermute | solution.py:23
  87.9 20.3 %collective-permute-start.27 = (bf16[256,1536]{1,0:T(8,128)(2,1)S(1)}, bf16[256,1536]{1,0:T(8,128)(2,1)S(1)}, u32[]{:S(2)}, u32[]{:S(2)}) collective-permute-start(bf16[256,1536]{1,0:T(8,128)(2,1)S(1)} %convolution_convert_fusion), channel_id=1, source_target_pairs={{0,12},{1,13},{2,14},{3,15},{4,8},{5,9},{6,10},{7,11},{8,4},{9,5},... | collective-permute-start | bytes 2359304 | tf_op jit(solution)/shard_map/ppermute | solution.py:23
  90.2 19.8 %collective-permute-start.22 = (bf16[256,1536]{1,0:T(8,128)(2,1)S(1)}, bf16[256,1536]{1,0:T(8,128)(2,1)S(1)}, u32[]{:S(2)}, u32[]{:S(2)}) collective-permute-start(bf16[256,1536]{1,0:T(8,128)(2,1)S(1)} %convolution_convert_fusion.2), channel_id=1, source_target_pairs={{0,1},{1,0},{2,3},{3,2},{4,5},{5,4},{6,7},{7,6},{8,9},{9,8},{10,11... | collective-permute-start | bytes 2359304 | tf_op jit(solution)/shard_map/ppermute | solution.py:23
  92.2 38.8 %collective-permute-start.26 = (bf16[256,1536]{1,0:T(8,128)(2,1)S(1)}, bf16[256,1536]{1,0:T(8,128)(2,1)S(1)}, u32[]{:S(2)}, u32[]{:S(2)}) collective-permute-start(bf16[256,1536]{1,0:T(8,128)(2,1)S(1)} %convolution_convert_fusion.1), channel_id=1, source_target_pairs={{0,12},{1,13},{2,14},{3,15},{4,8},{5,9},{6,10},{7,11},{8,4},{9,5},... | collective-permute-start | bytes 2359304 | tf_op jit(solution)/shard_map/ppermute | solution.py:23
  93.5 13.2 %collective-permute-start.16 = (bf16[256,1536]{1,0:T(8,128)(2,1)S(1)}, bf16[256,1536]{1,0:T(8,128)(2,1)S(1)}, u32[]{:S(2)}, u32[]{:S(2)}) collective-permute-start(bf16[256,1536]{1,0:T(8,128)(2,1)S(1)} %convolution_convert_fusion.4), channel_id=1, source_target_pairs={{0,48},{1,49},{2,50},{3,51},{4,52},{5,53},{6,54},{7,55},{8,56},{9,... | collective-permute-start | bytes 2359304 | tf_op jit(solution)/shard_map/ppermute | solution.py:23
  106.7 13.2 %collective-permute-start.10 = (bf16[256,1536]{1,0:T(8,128)(2,1)S(1)}, bf16[256,1536]{1,0:T(8,128)(2,1)S(1)}, u32[]{:S(2)}, u32[]{:S(2)}) collective-permute-start(bf16[256,1536]{1,0:T(8,128)(2,1)S(1)} %convolution_convert_fusion.5), channel_id=1, source_target_pairs={{0,48},{1,49},{2,50},{3,51},{4,52},{5,53},{6,54},{7,55},{8,56},{9,... | collective-permute-start | bytes 2359304 | tf_op jit(solution)/shard_map/ppermute | solution.py:23
  108.3 9.1 %collective-permute-start.18 = (bf16[128,1536]{1,0:T(8,128)(2,1)S(1)}, bf16[128,1536]{1,0:T(8,128)(2,1)S(1)}, u32[]{:S(2)}, u32[]{:S(2)}) collective-permute-start(bf16[128,1536]{1,0:T(8,128)(2,1)S(1)} %get-tuple-element.12), channel_id=1, source_target_pairs={{0,12},{1,13},{2,14},{3,15},{4,8},{5,9},{6,10},{7,11},{8,4},{9,5},... | collective-permute-start | bytes 1179656 | tf_op jit(solution)/shard_map/ppermute | solution.py:23
  110.0 32.3 %collective-permute-start.28 = (bf16[128,1536]{1,0:T(8,128)(2,1)S(1)}, bf16[128,1536]{1,0:T(8,128)(2,1)S(1)}, u32[]{:S(2)}, u32[]{:S(2)}) collective-permute-start(bf16[128,1536]{1,0:T(8,128)(2,1)S(1)} %get-tuple-element.15), channel_id=1, source_target_pairs={{0,1},{1,0},{2,3},{3,2},{4,5},{5,4},{6,7},{7,6},{8,9},{9,8},{10,11... | collective-permute-start | bytes 1179656 | tf_op jit(solution)/shard_map/ppermute | solution.py:23
  117.3 15.0 %collective-permute-start.29 = (bf16[128,1536]{1,0:T(8,128)(2,1)S(1)}, bf16[128,1536]{1,0:T(8,128)(2,1)S(1)}, u32[]{:S(2)}, u32[]{:S(2)}) collective-permute-start(bf16[128,1536]{1,0:T(8,128)(2,1)S(1)} %get-tuple-element.16), channel_id=1, source_target_pairs={{0,1},{1,0},{2,3},{3,2},{4,5},{5,4},{6,7},{7,6},{8,9},{9,8},{10,11... | collective-permute-start | bytes 1179656 | tf_op jit(solution)/shard_map/ppermute | solution.py:23
  121.2 14.7 %collective-permute-start.23 = (bf16[128,1536]{1,0:T(8,128)(2,1)S(1)}, bf16[128,1536]{1,0:T(8,128)(2,1)S(1)}, u32[]{:S(2)}, u32[]{:S(2)}) collective-permute-start(bf16[128,1536]{1,0:T(8,128)(2,1)S(1)} %get-tuple-element.13), channel_id=1, source_target_pairs={{0,48},{1,49},{2,50},{3,51},{4,52},{5,53},{6,54},{7,55},{8,56},{9,... | collective-permute-start | bytes 1179656 | tf_op jit(solution)/shard_map/ppermute | solution.py:23
  128.9 13.8 %collective-permute-start.17 = (bf16[128,1536]{1,0:T(8,128)(2,1)S(1)}, bf16[128,1536]{1,0:T(8,128)(2,1)S(1)}, u32[]{:S(2)}, u32[]{:S(2)}) collective-permute-start(bf16[128,1536]{1,0:T(8,128)(2,1)S(1)} %get-tuple-element.11), channel_id=1, source_target_pairs={{0,12},{1,13},{2,14},{3,15},{4,8},{5,9},{6,10},{7,11},{8,4},{9,5},... | collective-permute-start | bytes 1179656 | tf_op jit(solution)/shard_map/ppermute | solution.py:23
  131.0 11.1 %collective-permute-start.25 = (bf16[128,1536]{1,0:T(8,128)(2,1)S(1)}, bf16[128,1536]{1,0:T(8,128)(2,1)S(1)}, u32[]{:S(2)}, u32[]{:S(2)}) collective-permute-start(bf16[128,1536]{1,0:T(8,128)(2,1)S(1)} %fusion.7), channel_id=1, source_target_pairs={{0,12},{1,13},{2,14},{3,15},{4,8},{5,9},{6,10},{7,11},{8,4},{9,5},... | collective-permute-start | bytes 1179656 | tf_op jit(solution)/shard_map/ppermute | solution.py:23
  (12 other events, 87.5 us)
